TPU v7x, 256 devices: a 2x2x32 block of a 4x8x32 slice. The times are simulated.
256 devices in a mesh: rep: 4 (over x, y), ctx: 64 (over z, core).
Axes of the slice: x: 2, y: 2, z: 32, core: 2. Of those that a mesh axis runs over, the one named last changes fastest.
The devices are a block of a 4x8x32 slice.
Arguments:
- queries: bfloat16 [32768, 32, 128], P(('rep', 'ctx')), parts along dimension 0, may hold values from -128 to 128
- keys: bfloat16 [32768, 2, 128], P(('rep', 'ctx')), parts along dimension 0, may hold values from -5 to 5
- values: bfloat16 [32768, 2, 128], P(('rep', 'ctx')), parts along dimension 0, may hold values from -6 to 6
- grad_out: bfloat16 [32768, 32, 128], P(('rep', 'ctx')), parts along dimension 0, may hold values from -6 to 6
- selected: int32 [32768, 2, 8], P(('rep', 'ctx')), parts along dimension 0, may hold values from 0 to 127, as said below
Outputs:
- dquery: bfloat16 [32768, 32, 128], P(('rep', 'ctx')), parts along dimension 0
- key_grad: bfloat16 [32768, 2, 128], P(('rep', 'ctx')), parts along dimension 0
- value_grad: bfloat16 [32768, 2, 128], P(('rep', 'ctx')), parts along dimension 0
There are 4 independent parts, one for each index of `rep`. A program takes and returns all parts, laid end to end along the dimension named above; each array names one. Nothing has to cross between parts.
Inputs may be any that keep to these rules, and one draw needn't show every extreme that they name: The 8 blocks of selected[t, g] are different and include block t // 64 and block 0. Over the 128 tokens of one device of ctx, the blocks named for one group that lie on other devices number exactly 7, at most one of each other device; block 0 is among them for every device but the first.
All inputs are finite; a program needn't handle non-finite values.
Results may differ from a plain program's by a relative error of at most 0.0075.
Values may be sent and summed in bfloat16 or wider, within the bound.
A program may use at most 128 MiB of HBM per device.

v0:
```python
import math

import jax
import jax.numpy as jnp
from jax import lax
from jax.sharding import PartitionSpec as P

BLK = 64


def side_by_side(arrays, axis, split_dim, concat_dim, along):
    widths = [a.shape[along] for a in arrays]
    both = jnp.concatenate(arrays, axis=along)
    result = lax.all_to_all(both, axis, split_axis=split_dim, concat_axis=concat_dim, tiled=True)
    return tuple(jnp.split(result, [sum(widths[:k]) for k in range(1, len(widths))], axis=along))


def attend_group(query_grp, upstream_grp, pool_keys, pool_values, allowed, block_rows):
    tokens, per_group, head_dim = query_grp.shape
    key_count = pool_keys.shape[0]
    scaling = 1.0 / math.sqrt(head_dim)
    step_count = tokens // block_rows
    query_blocks = query_grp.reshape(step_count, block_rows * per_group, head_dim)
    upstream_blocks = upstream_grp.reshape(step_count, block_rows * per_group, head_dim)
    mask_blocks = allowed.reshape(step_count, block_rows, key_count)
    contract_rows = (((0,), (0,)), ((), ()))
    contract_last = (((1,), (1,)), ((), ()))

    def visit(carry, inputs):
        key_acc, value_acc = carry
        query_rows, upstream_rows, mask_rows = inputs
        scores = lax.dot_general(
            query_rows, pool_keys, contract_last, preferred_element_type=jnp.float32
        )
        scores = scores.reshape(block_rows, per_group, key_count) * scaling
        scores = jnp.where(mask_rows[:, None, :], scores, -jnp.inf)
        row_peak = jnp.max(scores, axis=-1, keepdims=True)
        weights = jnp.exp(scores - row_peak)
        weights = weights / jnp.sum(weights, axis=-1, keepdims=True)
        slope_grad = lax.dot_general(
            upstream_rows, pool_values, contract_last, preferred_element_type=jnp.float32
        )
        slope_grad = slope_grad.reshape(block_rows, per_group, key_count)
        row_inner = jnp.sum(weights * slope_grad, axis=-1, keepdims=True)
        dscore = (weights * (slope_grad - row_inner) * scaling).astype(jnp.bfloat16)
        dscore = dscore.reshape(block_rows * per_group, key_count)
        weights_low = weights.astype(jnp.bfloat16).reshape(block_rows * per_group, key_count)
        dquery = jnp.dot(dscore, pool_keys, preferred_element_type=jnp.float32).astype(jnp.bfloat16)
        key_acc = key_acc + lax.dot_general(
            dscore, query_rows, contract_rows, preferred_element_type=jnp.float32
        )
        value_acc = value_acc + lax.dot_general(
            weights_low, upstream_rows, contract_rows, preferred_element_type=jnp.float32
        )
        return ((key_acc, value_acc), dquery)

    zeros_init = jnp.zeros((key_count, head_dim), jnp.float32)
    (key_acc, value_acc), dquery = lax.scan(
        visit, (zeros_init, zeros_init), (query_blocks, upstream_blocks, mask_blocks)
    )
    return (dquery.reshape(tokens, per_group, head_dim), key_acc, value_acc)


def local(queries, keys, values, grad_out, selected):
    tokens, head_count, head_dim = queries.shape
    groups = keys.shape[1]
    per_group = head_count // groups
    block_len = BLK
    own_blocks = tokens // block_len
    owners = lax.axis_size("ctx")
    fetched = min(owners - 2, max(selected.shape[2] - own_blocks, 4)) + 1
    block_rows = min(tokens, 128)
    my_index = lax.axis_index("ctx")
    peer_ids = jnp.arange(owners)
    owner_of = selected // own_blocks
    local_of = selected % own_blocks
    matches = owner_of[..., None] == peer_ids
    wanted = jnp.any(matches, axis=(0, 2)) & (peer_ids[None, :] != my_index)
    local_ids = jnp.max(jnp.where(matches, local_of[..., None], 0), axis=(0, 2))
    block_table = local_ids.T
    live_table = wanted.T.astype(jnp.int32)
    asked_block, asked_live = side_by_side((block_table, live_table), "ctx", 0, 0, 1)
    stacked = jnp.stack([keys, values], axis=2)
    own_items = stacked.reshape(own_blocks, block_len, groups, 2, head_dim).transpose(0, 2, 3, 1, 4)
    whole_kv = lax.all_gather(stacked, "ctx", axis=0, tiled=True)
    whole_kv = whole_kv.reshape(-1, block_len, groups, 2, head_dim)
    query_pos = my_index * tokens + jnp.arange(tokens)
    own_ids = my_index * own_blocks + jnp.arange(own_blocks)
    dquery_parts = []
    own_grads = []
    back_parts = []
    for group in range(groups):
        is_live = wanted[group]
        slot_pos = jnp.cumsum(is_live.astype(jnp.int32)) - 1
        picker = (slot_pos[None, :] == jnp.arange(fetched)[:, None]) & is_live[None, :]
        far_blocks = jnp.sum(
            jnp.where(picker, peer_ids[None, :] * own_blocks + local_ids[group][None, :], 0), axis=1
        )
        fetched_kv = whole_kv[:, :, group][far_blocks].transpose(0, 2, 1, 3)
        pool_kv = jnp.concatenate([own_items[:, group], fetched_kv], axis=0)
        pool_blocks = jnp.concatenate([own_ids, far_blocks], axis=0)
        pool_keys = pool_kv[:, 0].reshape(-1, head_dim)
        pool_values = pool_kv[:, 1].reshape(-1, head_dim)
        key_pos = (pool_blocks[:, None] * block_len + jnp.arange(block_len)[None, :]).reshape(-1)
        picked = jnp.any(selected[:, group, :, None] == pool_blocks[None, None, :], axis=1)
        allowed = jnp.repeat(picked, block_len, axis=1) & (key_pos[None, :] <= query_pos[:, None])
        lower = group * per_group
        dquery, key_acc, value_acc = attend_group(
            queries[:, lower : lower + per_group],
            grad_out[:, lower : lower + per_group],
            pool_keys,
            pool_values,
            allowed,
            block_rows,
        )
        pool_grads = (
            jnp.stack([key_acc, value_acc], axis=0)
            .reshape(2, -1, block_len, head_dim)
            .transpose(1, 0, 2, 3)
        )
        own_grads.append(pool_grads[:own_blocks])
        back_parts.append(
            jnp.dot(picker.astype(jnp.float32).T, pool_grads[own_blocks:].reshape(fetched, -1))
        )
        dquery_parts.append(dquery)
    outgoing = jnp.stack(back_parts, axis=1).reshape(owners, groups, 2, block_len, head_dim)
    returned = lax.all_to_all(outgoing, "ctx", split_axis=0, concat_axis=0, tiled=True)
    collected = []
    for group in range(groups):
        senders = (asked_block[:, group][None, :] == jnp.arange(own_blocks)[:, None]) & (
            asked_live[:, group][None, :] > 0
        )
        summed = jnp.dot(senders.astype(jnp.float32), returned[:, group].reshape(owners, -1))
        collected.append(summed.reshape(own_blocks, 2, block_len, head_dim) + own_grads[group])
    summed_all = jnp.stack(collected, axis=1)
    key_grad = (
        summed_all[:, :, 0]
        .transpose(0, 2, 1, 3)
        .reshape(tokens, groups, head_dim)
        .astype(jnp.bfloat16)
    )
    value_grad = (
        summed_all[:, :, 1]
        .transpose(0, 2, 1, 3)
        .reshape(tokens, groups, head_dim)
        .astype(jnp.bfloat16)
    )
    dquery_all = jnp.concatenate(dquery_parts, axis=1)
    return (dquery_all, key_grad, value_grad)


def solution(mesh):
    return jax.shard_map(
        local,
        mesh=mesh,
        in_specs=(
            P(("rep", "ctx"), None, None),
            P(("rep", "ctx"), None, None),
            P(("rep", "ctx"), None, None),
            P(("rep", "ctx"), None, None),
            P(("rep", "ctx"), None, None),
        ),
        out_specs=(
            P(("rep", "ctx"), None, None),
            P(("rep", "ctx"), None, None),
            P(("rep", "ctx"), None, None),
        ),
        check_vma=False,
    )
```

profile of v0, /device:TPU:38, one launch (start us, length us, event | category | flops | bytes accessed | tf_op | source)
XLA Modules:
  0.0 710.2 jit_solution(354019494511695271)
XLA Ops:
  10.7 34.4 %all-to-all-start = ((s32[64,1,4]{2,1,0:T(1,128)}), s32[64,1,4]{2,1,0:T(1,128)S(1)}, u32[]{:S(2)}, u32[]{:S(2)}) async-start(s32[64,1,4]{2,1,0:T(1,128)} %bitcast.44), calls=%async_computation | async-start | bytes 65536 | tf_op jit(solution)/shard_map/all_to_all | solution.py:14
  55.1 107.3 %all-gather.2.cloned.1.call-done = bf16[8192,2,2,128]{3,0,2,1:T(8,128)(2,1)} async-done(((bf16[128,2,2,128]{3,0,2,1:T(8,128)(2,1)}), bf16[8192,2,2,128]{3,0,2,1:T(8,128)(2,1)}) %all-gather.2.cloned.1.call-update) | async-done | bytes 8388624 | tf_op jit(solution)/shard_map/all_gather | solution.py:85
  162.4 5.8 fusion.77
  171.1 3.4 gather_fusion.1
  180.0 3.4 fusion.7
  183.4 6.0 copy.274
  189.4 5.5 copy.349
  194.9 3.4 gather_fusion
  207.9 5.8 copy.267
  214.4 6.2 multiply_reduce_fusion
  221.3 5.8 copy.275
  227.1 6.7 fusion.9
  233.7 5.2 copy.276
  242.1 5.6 copy.278
  254.2 6.2 multiply_reduce_fusion.1
  261.2 5.8 copy.268
  267.0 6.7 fusion.8
  273.7 5.2 copy.269
  282.0 5.2 copy.271
  292.9 4.6 copy.281
  297.6 14.7 %all-to-all-start.1 = ((bf16[64,2,2,64,128]{4,3,2,1,0:T(8,128)(2,1)}), bf16[64,2,2,64,128]{4,3,2,1,0:T(8,128)(2,1)}, u32[]{:S(2)}, u32[]{:S(2)}) async-start(bf16[64,2,2,64,128]{4,3,2,1,0:T(8,128)(2,1)} %copy.281), calls=%async_computation.1 | async-start | bytes 8388608 | tf_op jit(solution)/shard_map/all_to_all | solution.py:127
  313.7 6.0 convolution_convert_fusion
  319.8 4.5 convolution_convert_fusion.1
  325.3 365.9 %all-to-all-done.1 = bf16[64,2,2,64,128]{4,3,2,1,0:T(8,128)(2,1)} async-done(((bf16[64,2,2,64,128]{4,3,2,1,0:T(8,128)(2,1)}), bf16[64,2,2,64,128]{4,3,2,1,0:T(8,128)(2,1)}, u32[]{:S(2)}, u32[]{:S(2)}) %all-to-all-start.1) | async-done | bytes 4194336 | tf_op jit(solution)/shard_map/all_to_all | solution.py:127
  (130 shorter events, 66.0 us)
Async XLA Ops:
  7.2 155.2 %all-gather.2.cloned.1.call-start = ((), (), s32[]{:S(2)}) async-start(), calls=%async_computation.2 | async-start | bytes 8519680 | tf_op jit(solution)/shard_map/all_gather | solution.py:85
  10.7 286.9 %all-to-all-start = ((s32[64,1,4]{2,1,0:T(1,128)}), s32[64,1,4]{2,1,0:T(1,128)S(1)}, u32[]{:S(2)}, u32[]{:S(2)}) async-start(s32[64,1,4]{2,1,0:T(1,128)} %bitcast.44), calls=%async_computation | async-start | bytes 65536 | tf_op jit(solution)/shard_map/all_to_all | solution.py:14
  45.1 6.7 copy-start.12
  45.7 0.6 copy-start.10
  47.9 3.9 copy-start.3
  48.2 3.7 copy-start.4
  48.5 5.4 copy-start.2
  176.2 0.7 copy-start.5
  200.0 0.7 copy-start.6
  242.1 5.7 copy-start.9
  282.0 5.2 copy-start.8
  287.3 4.5 copy-start.11
  287.3 4.5 copy-start.13
  287.3 5.3 copy-start
  290.9 0.9 copy-start.1
  297.6 22.2 %slice-start = ((s8[4718592]{0:T(1024)(128)(4,1)}), s8[524288]{0:T(1024)(128)(4,1)S(1)}, s32[]{:S(2)}) async-start(s8[4718592]{0:T(1024)(128)(4,1)} %bitcast.214), calls=%async_computation.3 | async-start | bytes 1048576
  297.6 393.6 %all-to-all-start.1 = ((bf16[64,2,2,64,128]{4,3,2,1,0:T(8,128)(2,1)}), bf16[64,2,2,64,128]{4,3,2,1,0:T(8,128)(2,1)}, u32[]{:S(2)}, u32[]{:S(2)}) async-start(bf16[64,2,2,64,128]{4,3,2,1,0:T(8,128)(2,1)} %copy.281), calls=%async_computation.1 | async-start | bytes 8388608 | tf_op jit(solution)/shard_map/all_to_all | solution.py:127
  313.7 6.0 slice-start.1
  313.7 6.0 copy-start.7
  694.3 2.0 copy-start.16
  694.3 2.0 copy-start.17
  697.6 2.9 copy-start.14
  697.6 2.9 copy-start.15
Sparse Core Ops, SparseCore 0:
  9.9 152.4 all-gather.1
where the time goes:
time: 715 us; the launch traced here: 710 us
  waiting for transfers between devices  473 us (66%)
  local copies, waits for them, and re-layouts  95.8 us (13%)
  starting transfers between devices  49.2 us (7%)
  matrix products  45.7 us (6%)
  other arithmetic  31.6 us (4%)
  between operations  14.8 us (2%)
    all_to_all x1, waiting for transfers between devices, local(): lax.all_to_all(outgoing, 'ctx', split_axis=0, concat_axis=0, tiled=True)  366 us
    all_gather x1, waiting for transfers between devices, local(): whole_kv = lax.all_gather(stacked, 'ctx', axis=0, tiled=True)  107 us
    all_to_all x1, starting transfers between devices, side_by_side(): lax.all_to_all(both, axis, split_axis=split_dim, concat_axis=concat_dim,...  34.4 us
    all_to_all x1, starting transfers between devices, local(): lax.all_to_all(outgoing, 'ctx', split_axis=0, concat_axis=0, tiled=True)  14.7 us
  transfers between devices with their start and end apart: 3, of which 2 were waited for; matrix products, arithmetic and copies ran while one was open for 22% of the time, Pallas kernels for 0%

commit v1 on v0

v1 whole, which is shorter than its diff:
```python
import functools
import math

import jax
import jax.numpy as jnp
from jax import lax
from jax.experimental import pallas as pl
from jax.experimental.pallas import tpu as pltpu
from jax.sharding import PartitionSpec as P

BLK = 64
CORES = 2
NEG = -1e30
MESH = pl.DeviceIdType.MESH
CHUNKS = 2


def remote(src, dst, send_sem, recv_sem, target):
    return pltpu.make_async_remote_copy(
        src_ref=src,
        dst_ref=dst,
        send_sem=send_sem,
        recv_sem=recv_sem,
        device_id={"ctx": target},
        device_id_type=MESH,
    )


def ring_ids(chips):
    me = lax.axis_index("ctx")
    chip, core = me // CORES, lax.rem(me, CORES)
    above = lax.rem(chip + 1, chips) * CORES + core
    below = lax.rem(chip + chips - 1, chips) * CORES + core
    sibling = chip * CORES + (1 - core)
    return me, chip, core, above, below, sibling


def greet(above, below, sibling):
    barrier = pltpu.get_barrier_semaphore()
    for peer in (above, below, sibling):
        pl.semaphore_signal(barrier, inc=1, device_id={"ctx": peer}, device_id_type=MESH)
    pl.semaphore_wait(barrier, 3)


def gather_kernel(
    chips, far_owner, far_local, unit_ref, table_ref, picked_ref, other_ref,
    pool, other, up_send, up_recv, dn_send, dn_recv, sib_send, sib_recv, tab_sem,
):
    me, chip, core, above, below, sibling = ring_ids(chips)
    groups = unit_ref.shape[0]
    far = far_owner.shape[1]
    n_up, n_dn = chips // 2, chips - 1 - chips // 2
    greet(above, below, sibling)

    def owner_up(step):
        return lax.rem(chip + chips - step, chips) * CORES + core

    def owner_dn(step):
        return lax.rem(chip + step, chips) * CORES + core

    def up_copy(step, part, src, owner):
        return remote(
            src, pool.at[owner, part], up_send.at[step, part], up_recv.at[step, part], above
        )

    def dn_copy(step, part, src, owner):
        return remote(
            src, pool.at[owner, part], dn_send.at[step, part], dn_recv.at[step, part], below
        )

    def sib_copy(slot, part, src, owner):
        return remote(
            src, pool.at[owner, part], sib_send.at[slot, part], sib_recv.at[slot, part], sibling
        )

    for part in range(groups):
        up_copy(0, part, unit_ref.at[part], me).start()
        dn_copy(0, part, unit_ref.at[part], me).start()
        sib_copy(0, part, unit_ref.at[part], me).start()
    tab_copy = remote(table_ref, other, tab_sem.at[0], tab_sem.at[1], sibling)
    tab_copy.start()
    pool[me] = unit_ref[...]

    def step_up(step, last):
        owner = owner_up(step)
        for part in range(groups):
            up_copy(step - 1, part, pool.at[owner, part], owner).wait_recv()
            if not last:
                up_copy(step, part, pool.at[owner, part], owner).start()
            sib_copy(step, part, pool.at[owner, part], owner).start()

    def step_dn(step, last):
        owner = owner_dn(step)
        for part in range(groups):
            dn_copy(step - 1, part, pool.at[owner, part], owner).wait_recv()
            if not last:
                dn_copy(step, part, pool.at[owner, part], owner).start()
            sib_copy(n_up + step, part, pool.at[owner, part], owner).start()

    @pl.loop(1, n_dn)
    def _(step):
        step_up(step, False)
        step_dn(step, False)

    step_up(n_dn, False)
    step_dn(n_dn, True)
    step_up(n_up, True)

    @pl.loop(0, chips)
    def _(slot):
        for part in range(groups):
            sib_copy(slot, part, unit_ref.at[part], me).wait_recv()
            sib_copy(slot, part, unit_ref.at[part], me).wait_send()

    @pl.loop(0, n_up)
    def _(step):
        for part in range(groups):
            up_copy(step, part, unit_ref.at[part], me).wait_send()

    @pl.loop(0, n_dn)
    def _(step):
        for part in range(groups):
            dn_copy(step, part, unit_ref.at[part], me).wait_send()

    tab_copy.wait()
    other_ref[...] = other[...]
    picked_ref[:, :, 0:2] = unit_ref[...]
    for group in range(groups):
        for slot in range(far):
            picked_ref[group, :, 2 + slot] = pool[
                far_owner[group, slot], group, :, far_local[group, slot]
            ]


def attend_kernel(heads, q_ref, g_ref, kv_ref, vis_ref, dq_ref, grads_ref):
    tile = pl.program_id(1)
    tokens, _, dim = q_ref.shape
    slots, blk = kv_ref.shape[2], kv_ref.shape[3]
    own = 2
    cols = tokens * heads
    scaling = 1.0 / math.sqrt(dim)
    query = q_ref[...].reshape(cols, dim)
    upstream = g_ref[...].reshape(cols, dim)
    keys = kv_ref[0, 0].reshape(slots * blk, dim)
    values = kv_ref[0, 1].reshape(slots * blk, dim)
    last = (((1,), (1,)), ((), ()))
    all_tok = vis_ref.shape[2]
    row_tok = lax.broadcasted_iota(jnp.int32, (all_tok, cols), 0)
    col_tok = lax.broadcasted_iota(jnp.int32, (all_tok, cols), 1) // heads + tile * tokens
    spread = (row_tok == col_tok).astype(jnp.bfloat16)
    seen = jnp.dot(vis_ref[0], spread, preferred_element_type=jnp.float32)
    bias = (seen - 1.0) * (-NEG)
    scores = lax.dot_general(keys, query, last, preferred_element_type=jnp.float32)
    scores = scores * (scaling * math.log2(math.e))
    key_pos = lax.broadcasted_iota(jnp.int32, (own * blk, cols), 0)
    tok_pos = lax.broadcasted_iota(jnp.int32, (own * blk, cols), 1) // heads + tile * tokens
    causal = jnp.where(key_pos <= tok_pos, 0.0, NEG)
    pieces = []
    for slot in range(slots):
        piece = scores[slot * blk : (slot + 1) * blk] + bias[slot : slot + 1]
        if slot < own:
            piece = piece + causal[slot * blk : (slot + 1) * blk]
        pieces.append(piece)
    scores = jnp.concatenate(pieces, axis=0)
    peak = jnp.max(scores, axis=0, keepdims=True)
    weights = jnp.exp2(scores - peak)
    weights = weights * (1.0 / jnp.sum(weights, axis=0, keepdims=True))
    slope = lax.dot_general(values, upstream, last, preferred_element_type=jnp.float32)
    inner = jnp.sum(weights * slope, axis=0, keepdims=True)
    dscore = (weights * (slope - inner) * scaling).astype(jnp.bfloat16)
    low = weights.astype(jnp.bfloat16)
    dquery = lax.dot_general(
        dscore, keys, (((0,), (0,)), ((), ())), preferred_element_type=jnp.float32
    )
    dq_ref[...] = dquery.astype(jnp.bfloat16).reshape(tokens, heads, dim)
    key_part = jnp.dot(dscore, query, preferred_element_type=jnp.float32)
    value_part = jnp.dot(low, upstream, preferred_element_type=jnp.float32)

    @pl.when(tile == 0)
    def _():
        grads_ref[...] = jnp.zeros_like(grads_ref)

    grads_ref[0, 0, 0:slots] += key_part.reshape(slots, blk, dim)
    grads_ref[0, 1, 0:slots] += value_part.reshape(slots, blk, dim)


def scatter_kernel(
    chips, mine, theirs, grads_ref, out_ref,
    sib, up, dn, up_send, up_recv, dn_send, dn_recv, sib_sem,
):
    me, chip, core, above, below, sibling = ring_ids(chips)
    groups = grads_ref.shape[0]
    own = 2
    n_dn, n_up = chips // 2, chips - 1 - chips // 2
    greet(above, below, sibling)
    swap = remote(grads_ref, sib, sib_sem.at[0], sib_sem.at[1], sibling)
    swap.start()
    swap.wait()

    def local_sum(owner, group, local):
        block = owner * own + local
        a = mine[group, block]
        b = theirs[group, block]
        return grads_ref[group, :, own + a] + sib[group, :, own + b]

    def dn_copy(step, part):
        return remote(
            dn.at[step, part], dn.at[step + 1, part],
            dn_send.at[step, part], dn_recv.at[step, part], below,
        )

    def up_copy(step, part):
        return remote(
            up.at[step, part], up.at[step + 1, part],
            up_send.at[step, part], up_recv.at[step, part], above,
        )

    def dn_owner(step):
        return lax.rem(chip + 2 * chips - n_dn + step, chips) * CORES + core

    def up_owner(step):
        return lax.rem(chip + n_up - step, chips) * CORES + core

    for group in range(groups):
        for buf, owner, copy in ((dn, dn_owner(0), dn_copy), (up, up_owner(0), up_copy)):
            for local in range(own):
                buf[0, group, :, local] = local_sum(owner, group, local).astype(buf.dtype)
            copy(0, group).start()

    def advance(buf, owner, copy, step):
        for group in range(groups):
            copy(step - 1, group).wait_recv()
            for local in range(own):
                total = buf[step, group, :, local].astype(jnp.float32)
                total = total + local_sum(owner, group, local)
                buf[step, group, :, local] = total.astype(buf.dtype)
            copy(step, group).start()

    @pl.loop(1, n_up)
    def _(step):
        advance(dn, dn_owner(step), dn_copy, step)
        advance(up, up_owner(step), up_copy, step)

    @pl.loop(n_up, n_dn)
    def _(step):
        advance(dn, dn_owner(step), dn_copy, step)

    for group in range(groups):
        dn_copy(n_dn - 1, group).wait_recv()
        up_copy(n_up - 1, group).wait_recv()
        for local in range(own):
            b = theirs[group, me * own + local]
            total = dn[n_dn, group, :, local].astype(jnp.float32)
            total = total + up[n_up, group, :, local].astype(jnp.float32)
            total = total + grads_ref[group, :, local] + sib[group, :, own + b]
            out_ref[group, :, local] = total.astype(out_ref.dtype)

    @pl.loop(0, n_up)
    def _(step):
        for group in range(groups):
            dn_copy(step, group).wait_send()
            up_copy(step, group).wait_send()

    @pl.loop(n_up, n_dn)
    def _(step):
        for group in range(groups):
            dn_copy(step, group).wait_send()


def local(queries, keys, values, grad_out, selected):
    tokens, head_count, dim = queries.shape
    groups = keys.shape[1]
    heads = head_count // groups
    owners = lax.axis_size("ctx")
    chips = owners // CORES
    own = tokens // BLK
    blocks = owners * own
    far = min(owners - 2, max(selected.shape[2] - own, 4)) + 1
    slots = own + far
    me = lax.axis_index("ctx")
    vmem = pl.BlockSpec(memory_space=pltpu.VMEM)
    smem = pl.BlockSpec(memory_space=pltpu.SMEM)

    unit = jnp.stack([keys, values], axis=0).transpose(2, 0, 1, 3)
    unit = unit.reshape(groups, 2, own, BLK, dim)
    sel = selected.transpose(1, 2, 0)
    block_ids = jnp.arange(blocks)
    named = jnp.any(sel[:, :, None, :] == block_ids[None, None, :, None], axis=1)
    is_far = jnp.any(named, axis=2) & (block_ids[None, :] // own != me)
    lower = (block_ids[:, None] <= block_ids[None, :]).astype(jnp.bfloat16)
    place = jnp.dot(is_far.astype(jnp.bfloat16), lower, preferred_element_type=jnp.float32)
    place = place.astype(jnp.int32) - 1
    table = jnp.where(is_far, place, far)
    picker = table[:, None, :] == jnp.arange(far)[None, :, None]
    far_block = jnp.sum(jnp.where(picker, block_ids[None, None, :], 0), axis=2)
    early = (block_ids // own < me)[None, None, :] & picker
    own_pick = block_ids[None, :] == me * own + jnp.arange(own)[:, None]
    rows = jnp.concatenate([jnp.broadcast_to(own_pick, (groups, own, blocks)), early], axis=1)
    rows = jnp.pad(rows, ((0, 0), (0, 16 - slots), (0, 0)))
    vis = jnp.einsum(
        "gsb,gbt->gst", rows.astype(jnp.bfloat16), named.astype(jnp.bfloat16),
        preferred_element_type=jnp.float32,
    ).astype(jnp.bfloat16)
    table8 = jnp.pad(table, ((0, 8 - groups), (0, 0)))

    n_half = chips // 2
    dma = pltpu.SemaphoreType.DMA
    picked, other = pl.pallas_call(
        functools.partial(gather_kernel, chips),
        out_shape=(
            jax.ShapeDtypeStruct((groups, 2, slots, BLK, dim), jnp.bfloat16),
            jax.ShapeDtypeStruct((8, blocks), jnp.int32),
        ),
        in_specs=[smem, smem, vmem, vmem],
        out_specs=(vmem, vmem),
        scratch_shapes=[
            pltpu.VMEM((owners, groups, 2, own, BLK, dim), jnp.bfloat16),
            pltpu.VMEM((8, blocks), jnp.int32),
            dma((n_half, groups)), dma((n_half, groups)),
            dma((n_half, groups)), dma((n_half, groups)),
            dma((chips, groups)), dma((chips, groups)),
            dma((2,)),
        ],
        compiler_params=pltpu.CompilerParams(collective_id=0, has_side_effects=True),
        name="gather_blocks",
    )(far_block // own, far_block % own, unit, table8)

    tile = 16
    steps = tokens // tile
    act = pl.BlockSpec((tile, heads, dim), lambda g, i: (i, g, 0))
    dquery, grads = pl.pallas_call(
        functools.partial(attend_kernel, heads),
        grid=(groups, steps),
        out_shape=(
            jax.ShapeDtypeStruct(queries.shape, jnp.bfloat16),
            jax.ShapeDtypeStruct((groups, 2, slots + 1, BLK, dim), jnp.float32),
        ),
        in_specs=[
            act, act,
            pl.BlockSpec((1, 2, slots, BLK, dim), lambda g, i: (g, 0, 0, 0, 0)),
            pl.BlockSpec((1, 16, tokens), lambda g, i: (g, 0, 0)),
        ],
        out_specs=(
            act,
            pl.BlockSpec((1, 2, slots + 1, BLK, dim), lambda g, i: (g, 0, 0, 0, 0)),
        ),
        name="attend_back",
    )(queries, grad_out, picked, vis)

    unit_shape = (groups, 2, own, BLK, dim)
    out = pl.pallas_call(
        functools.partial(scatter_kernel, chips),
        out_shape=jax.ShapeDtypeStruct(unit_shape, jnp.bfloat16),
        in_specs=[smem, smem, vmem],
        out_specs=vmem,
        scratch_shapes=[
            pltpu.VMEM((groups, 2, slots + 1, BLK, dim), jnp.float32),
            pltpu.VMEM((n_half + 1, *unit_shape), jnp.bfloat16),
            pltpu.VMEM((n_half + 1, *unit_shape), jnp.bfloat16),
            dma((n_half, groups)), dma((n_half, groups)),
            dma((n_half, groups)), dma((n_half, groups)),
            dma((2,)),
        ],
        compiler_params=pltpu.CompilerParams(collective_id=1, has_side_effects=True),
        name="scatter_sums",
    )(table, other[:groups], grads)
    both = out.transpose(1, 2, 3, 0, 4).reshape(2, tokens, groups, dim)
    return dquery, both[0], both[1]


def solution(mesh):
    spec = P(("rep", "ctx"), None, None)
    return jax.shard_map(
        local, mesh=mesh, in_specs=(spec,) * 5, out_specs=(spec,) * 3, check_vma=False
    )
```

time: 715 us -> 187 us (0.26)
  waiting for transfers between devices: 473 us -> 0 us
  Pallas kernels: 0 us -> 178 us
  local copies, waits for them, and re-layouts: 95.8 us -> 4.81 us
  starting transfers between devices: 49.2 us -> 0 us
  matrix products: 45.7 us -> 0.87 us
  other arithmetic: 31.6 us -> 2.81 us
  between operations: 14.8 us -> 0.68 us
    all_to_all x2 -> x0, waiting for transfers between devices: 366 us -> none  [the longest x1 366 us: local(): lax.all_to_all(outgoing, 'ctx', split_axis=0, concat_axis=0, tiled=True)]
    pallas_call x0 -> x3, Pallas kernels: none -> 178 us  [the longest x1 89.5 us: local(): pl.pallas_call(functools.partial(gather_kernel, chips), out_shape=(jax.Sh...]
    all_gather x1 -> x0, waiting for transfers between devices: 107 us -> none  [local(): whole_kv = lax.all_gather(stacked, 'ctx', axis=0, tiled=True)]
    all_to_all x2 -> x0, starting transfers between devices: 49.1 us -> none  [the longest x1 34.4 us: side_by_side(): lax.all_to_all(both, axis, split_axis=split_dim, concat_axis=concat_dim,...]
    dot_general x14 -> x2, matrix products: 45.7 us -> 0.87 us  [the longest x1 0.73 us: local(): jnp.einsum('gsb,gbt->gst', rows.astype(jnp.bfloat16), named.astype(jnp.bf...]
    dot_general x6 -> x0, local copies, waits for them, and re-layouts: 32.8 us -> none  [the longest x2 11.6 us: visit(): lax.dot_general(upstream_rows, pool_values, contract_last, preferred_elem...]
    slice x12 -> x2, local copies, waits for them, and re-layouts: 20.8 us -> 2.13 us  [the longest x1 1.25 us: local(): other[:groups]]
    dot_general x2 -> x0, other arithmetic: 13.4 us -> none  [visit(): lax.dot_general(dscore, query_rows, contract_rows, preferred_element_type...]
  transfers between devices with their start and end apart: 3 -> 0, of which waited for: 2 -> 0; matrix products, arithmetic and copies ran while one was open for 22% -> 0% of each run, Pallas kernels for 0% -> 0%
where the time goes in v1:
time: 187 us
  Pallas kernels  178 us (95%)
  local copies, waits for them, and re-layouts  4.81 us (3%)
  other arithmetic  2.81 us (2%)
    pallas_call x1, Pallas kernels, local(): pl.pallas_call(functools.partial(gather_kernel, chips), out_shape=(jax.Sh...  89.5 us
    pallas_call x1, Pallas kernels, local(): pl.pallas_call(functools.partial(scatter_kernel, chips), out_shape=jax.Sh...  69.2 us
    pallas_call x1, Pallas kernels, local(): pl.pallas_call(functools.partial(attend_kernel, heads), grid=(groups, ste...  19.2 us

profile of v1, /device:TPU:38, one launch (start us, length us, event | category | flops | bytes accessed | tf_op | source)
XLA Modules:
  0.0 187.1 jit_solution(16455831280374303870)
XLA Ops:
  0.6 0.1 iota_compare_fusion.4
  0.7 0.9 fusion.2
  1.6 0.1 fusion.1.mine
  1.8 0.0 copy-start
  1.8 0.1 select_reduce_fusion
  1.9 0.6 and_select_fusion
  2.5 0.7 convolution_convert_fusion.vis_ref
  3.3 0.6 pad.8.table_ref
  3.9 1.1 maximum_bitcast_fusion
  4.9 0.7 copy.11
  5.6 89.5 %gather_blocks.1 = (bf16[2,2,9,64,128]{4,3,2,1,0:T(8,128)(2,1)}, s32[8,128]{1,0:T(8,128)}) custom-call(s32[2,7]{1,0:T(2,128)} %get-tuple-element.22.far_owner, s32[2,7]{1,0:T(2,128)} %get-tuple-element.21.far_local, bf16[2,2,2,64,128]{4,3,2,1,0:T(8,128)(2,1)} %bitcast.10, s32[8,128]{1,0:T(8,128)} %pad.8.table_ref), custom_call_target="tpu_custom_call" | custom-call | tf_op jit(solution)/shard_map/gather_blocks/pallas_call | solution.py:308
  95.1 1.2 slice.11.theirs
  96.4 19.2 %attend_back.1 = (bf16[128,32,128]{2,1,0:T(8,128)(2,1)}, f32[2,2,10,64,128]{4,3,2,1,0:T(8,128)}) custom-call(bf16[128,32,128]{2,1,0:T(8,128)(2,1)} %q_ref.1, bf16[128,32,128]{2,1,0:T(8,128)(2,1)} %g_ref.1, bf16[2,2,9,64,128]{4,3,2,1,0:T(8,128)(2,1)} %get-tuple-element.7.kv_ref, bf16[2,16,128]{2,1,0:T(8,128)(2,1)} %convolution_convert_fusion.vis_ref), custom_call_target="tpu_custom_call" | custom-call | tf_op jit(solution)/shard_map/attend_back/pallas_call | solution.py:331
  115.6 0.0 copy-done
  115.6 69.2 %scatter_sums.1 = bf16[2,2,2,64,128]{4,3,2,1,0:T(8,128)(2,1)} custom-call(s32[2,128]{1,0:T(2,128)} %copy-done, s32[2,128]{1,0:T(2,128)} %slice.11.theirs, f32[2,2,10,64,128]{4,3,2,1,0:T(8,128)} %get-tuple-element.10.grads_ref), custom_call_target="tpu_custom_call" | custom-call | tf_op jit(solution)/shard_map/scatter_sums/pallas_call | solution.py:351
  184.8 0.9 fusion.9
  185.7 0.7 copy.13
  186.4 0.7 copy.12
  (5 shorter events, 0.0 us)
Async XLA Ops:
  1.8 113.8 %copy-start = (s32[2,128]{1,0:T(2,128)}, s32[2,128]{1,0:T(2,128)S(1)}, u32[]{:S(2)}) copy-start(s32[2,128]{1,0:T(2,128)S(1)} %fusion.1.mine) | copy-start | bytes 3076
